TPU v7x, 32 devices: a whole 2x2x4 slice. The times are simulated.
32 devices in a mesh: fsdp: 2 (over x), context: 4 (over z), tensor: 4 (over y, core).
Axes of the slice: x: 2, y: 2, z: 4, core: 2. Of those that a mesh axis runs over, the one named last changes fastest.
Arguments:
- activations: bfloat16 [2, 2048, 1152], P('fsdp', 'context'), may hold values from -6 to 6
- positions: int32 [2, 2048], P('fsdp', 'context'), may hold values from 0 to 2047, as said below
- seg_ids: int32 [2, 2048], P('fsdp', 'context'), may hold values from 0 to 3, as said below
- norm_gains: bfloat16 [4, 1152], P(None, ('fsdp', 'context')), may hold values from 0.5 to 1.5
- head_gains: bfloat16 [2, 256], P(None, ('fsdp', 'context')), may hold values from 0.25 to 1.75
- w_query: bfloat16 [1152, 1024], P(('fsdp', 'context'), 'tensor'), may hold values from -0.1875 to 0.1875
- w_keyval: bfloat16 [1152, 512], P(('fsdp', 'context')), may hold values from -0.1875 to 0.1875
- w_out: bfloat16 [1152, 1024], P(('fsdp', 'context'), 'tensor'), may hold values from -0.1875 to 0.1875
- w_gateup: bfloat16 [1152, 2, 6912], P(('fsdp', 'context'), None, 'tensor'), may hold values from -0.1875 to 0.1875
- w_down: bfloat16 [1152, 6912], P(('fsdp', 'context'), 'tensor'), may hold values from -0.078125 to 0.078125
- cotangent: bfloat16 [2, 2048, 1152], P('fsdp', 'context'), may hold values from -6 to 6
Outputs:
- block_output: bfloat16 [2, 2048, 1152], P('fsdp', 'context')
- input_grad: bfloat16 [2, 2048, 1152], P('fsdp', 'context')
- norm_gains_grad: float32 [4, 1152], P(None, ('fsdp', 'context'))
- head_gains_grad: float32 [2, 256], P(None, ('fsdp', 'context'))
- w_query_grad: float32 [1152, 1024], P(('fsdp', 'context'), 'tensor')
- w_keyval_grad: float32 [1152, 512], P(('fsdp', 'context'))
- w_out_grad: float32 [1152, 1024], P(('fsdp', 'context'), 'tensor')
- w_gateup_grad: float32 [1152, 2, 6912], P(('fsdp', 'context'), None, 'tensor')
- w_down_grad: float32 [1152, 6912], P(('fsdp', 'context'), 'tensor')
Inputs may be any that keep to these rules, and one draw needn't show every extreme that they name: `positions`: within a sequence, a document is a run of consecutive tokens with one document number; numbers never fall along a sequence. Positions are 0 at a document's first token and rise by one from token to token inside it. The first sequence is one document. `seg_ids`: document numbers of a sequence start at 0 and never fall along it.
All inputs are finite; a program needn't handle non-finite values.
Results may differ from a plain program's by a relative error of at most 0.024.
Values may be sent and summed in bfloat16 or wider, within the bound.
A program may use at most 192 MiB of HBM per device.

v0:
```python
import jax
import jax.numpy as jnp
from jax import lax
from jax.sharding import PartitionSpec as P

HD = 256
WINDOW = 512
EPSILON = 1e-06


def from_behind(block, axis, distance):
    devices = range(lax.axis_size(axis))
    route = [(i - distance, i) for i in devices if i - distance in devices]
    return lax.ppermute(block, axis, route)


def rms_norm(values, gain):
    factor = lax.rsqrt(jnp.mean(values * values, axis=-1, keepdims=True) + EPSILON)
    return values * factor * gain


def rotate(tensor, places):
    width_all = tensor.shape[-1]
    half_width = width_all // 2
    freqs = jnp.power(10000.0, -jnp.arange(half_width, dtype=jnp.float32) * 2.0 / width_all)
    angles = places.astype(jnp.float32)[:, None] * freqs[None, :]
    cosine = jnp.cos(angles)[:, None, :]
    sine = jnp.sin(angles)[:, None, :]
    first_half = tensor[..., :half_width]
    second_half = tensor[..., half_width:]
    return jnp.concatenate(
        [first_half * cosine - second_half * sine, second_half * cosine + first_half * sine],
        axis=-1,
    )


def glu(gate_up):
    return jax.nn.gelu(gate_up[:, 0], approximate=True) * gate_up[:, 1]


def contract_last(left_side, right_side):
    return lax.dot_general(
        left_side, right_side, (((1,), (1,)), ((), ())), preferred_element_type=jnp.float32
    )


def contract_first(left_side, right_side):
    return lax.dot_general(
        left_side, right_side, (((0,), (0,)), ((), ())), preferred_element_type=jnp.float32
    )


def shards(
    activations,
    positions,
    seg_ids,
    norm_gains,
    head_gains,
    w_query,
    w_keyval,
    w_out,
    w_gateup,
    w_down,
    cotangent,
):
    tokens = activations.shape[1]
    local_heads = w_query.shape[1] // HD
    inputs = activations[0].astype(jnp.float32)
    places = positions[0]
    documents = seg_ids[0]
    gains_all, heads_all, query_all, keyval_all, out_all = (
        lax.all_gather(norm_gains, ("fsdp", "context"), axis=1, tiled=True),
        lax.all_gather(head_gains, ("fsdp", "context"), axis=1, tiled=True),
        lax.all_gather(w_query, ("fsdp", "context"), axis=0, tiled=True),
        lax.all_gather(w_keyval, ("fsdp", "context"), axis=0, tiled=True),
        lax.all_gather(w_out, ("fsdp", "context"), axis=0, tiled=True),
    )
    gains_f = gains_all.astype(jnp.float32)
    heads_f = heads_all.astype(jnp.float32)
    normed_f, input_back = jax.vjp(rms_norm, inputs, gains_f[0])
    normed = normed_f.astype(jnp.bfloat16)
    query_raw = jnp.dot(normed, query_all, preferred_element_type=jnp.float32).reshape(
        tokens, local_heads, HD
    )
    keyval_raw = jnp.dot(normed, keyval_all, preferred_element_type=jnp.float32)

    def prepare(raw_heads, head_gain):
        return rotate(rms_norm(raw_heads, head_gain), places)

    query_rot, query_back = jax.vjp(prepare, query_raw, heads_f[0])
    key_rot, key_back = jax.vjp(prepare, keyval_raw[:, None, :HD], heads_f[1])
    queries = query_rot.astype(jnp.bfloat16)
    own_keyval = jnp.concatenate([key_rot[:, 0], keyval_raw[:, HD:]], axis=1).astype(jnp.bfloat16)
    labels = jnp.stack([places, documents])
    keep_from = tokens - tokens
    left_keyval, left_labels = from_behind((own_keyval, labels), "context", 1)
    keys_all = jnp.concatenate([left_keyval, own_keyval], axis=0)
    key_places = jnp.concatenate([left_labels[0], places])
    key_documents = jnp.concatenate([left_labels[1], documents])
    has_left = lax.axis_index("context") > 0
    key_live = jnp.concatenate([jnp.full((tokens,), has_left), jnp.ones((tokens,), dtype=bool)])
    scale_factor = HD ** (-0.5)
    block_rows = 512
    block_starts = jnp.arange(tokens // block_rows) * block_rows

    def block_scores():
        spacing = places[:, None] - key_places[None, :]
        visible = (
            key_live[None, :]
            & (documents[:, None] == key_documents[None, :])
            & (spacing >= 0)
            & (spacing < WINDOW)
        )
        raw_scores = (
            jnp.einsum("qhd,kd->hqk", queries, keys_all[:, :HD], preferred_element_type=jnp.float32)
            * scale_factor
        )
        return (jnp.where(visible[None], raw_scores, -1e30), keys_all, queries)

    def forward_block(start):
        scores, near_keyval, query_block = block_scores()
        row_top = jnp.max(scores, axis=-1, keepdims=True)
        raised = jnp.exp(scores - row_top)
        row_total = jnp.sum(raised, axis=-1, keepdims=True)
        probs = raised / row_total
        mixed_block = jnp.einsum(
            "hqk,kd->qhd",
            probs.astype(jnp.bfloat16),
            near_keyval[:, HD:],
            preferred_element_type=jnp.float32,
        )
        return (mixed_block.astype(jnp.bfloat16), row_top + jnp.log(row_total))

    mixed_blocks, log_blocks = lax.map(forward_block, block_starts)
    mixed_low = mixed_blocks.reshape(tokens, local_heads * HD)
    branch = lax.psum(contract_last(mixed_low, out_all).astype(jnp.bfloat16), "tensor").astype(
        jnp.float32
    )
    post_attn, post_attn_back = jax.vjp(rms_norm, branch, gains_f[1])
    hidden = inputs + post_attn
    normed_mlp_f, pre_mlp_back = jax.vjp(rms_norm, hidden, gains_f[2])
    normed_mlp = normed_mlp_f.astype(jnp.bfloat16)
    columns = normed_mlp
    gate_up = jnp.einsum(
        "bn,nkf->bkf",
        columns,
        lax.all_gather(w_gateup, ("fsdp", "context"), axis=0, tiled=True),
        preferred_element_type=jnp.float32,
    )
    active_f, glu_back = jax.vjp(glu, gate_up)
    active = active_f.astype(jnp.bfloat16)
    down = lax.psum(
        contract_last(
            active, lax.all_gather(w_down, ("fsdp", "context"), axis=0, tiled=True)
        ).astype(jnp.bfloat16),
        "tensor",
    ).astype(jnp.float32)
    post_mlp, post_mlp_back = jax.vjp(rms_norm, down, gains_f[3])
    result = hidden + post_mlp
    grad_out = cotangent[0].astype(jnp.float32)
    d_down, gain_post_mlp = post_mlp_back(grad_out)
    down_low = d_down.astype(jnp.bfloat16)
    columns = down_low
    d_active = jnp.dot(
        columns,
        lax.all_gather(w_down, ("fsdp", "context"), axis=0, tiled=True),
        preferred_element_type=jnp.float32,
    )
    d_gate_up = glu_back(d_active)[0].astype(jnp.bfloat16)
    d_normed_part = jnp.einsum(
        "bkf,nkf->bn",
        d_gate_up,
        lax.all_gather(w_gateup, ("fsdp", "context"), axis=0, tiled=True),
        preferred_element_type=jnp.float32,
    )
    d_normed_mlp = lax.psum(d_normed_part.astype(jnp.bfloat16), "tensor").astype(jnp.float32)
    d_hidden_norm, gain_pre_mlp = pre_mlp_back(d_normed_mlp)
    d_hidden = grad_out + d_hidden_norm
    features = normed_mlp
    grad_cols = down_low
    gate_up_term = jnp.einsum(
        "bn,bkf->nkf", features, d_gate_up, preferred_element_type=jnp.float32
    )
    down_term = contract_first(grad_cols, active)
    scatter = lambda part: lax.psum_scatter(
        part.astype(jnp.bfloat16), ("fsdp", "context"), scatter_dimension=0, tiled=True
    ).astype(jnp.float32)
    gate_grad = scatter(gate_up_term[:, 0])
    up_grad = scatter(gate_up_term[:, 1])
    down_grad = scatter(down_term)
    d_branch, gain_post_attn = post_attn_back(d_hidden)
    branch_low = d_branch.astype(jnp.bfloat16)
    d_mixed = jnp.dot(branch_low, out_all, preferred_element_type=jnp.float32)
    d_mixed_low = d_mixed.astype(jnp.bfloat16).reshape(tokens, local_heads, HD)

    def backward_block(carry, item):
        start, log_block = item
        scores, near_keyval, query_block = block_scores()
        probs_again = jnp.exp(scores - log_block)
        d_probs = jnp.einsum(
            "qhd,kd->hqk", d_mixed_low, near_keyval[:, HD:], preferred_element_type=jnp.float32
        )
        row_inner = jnp.sum(probs_again * d_probs, axis=-1, keepdims=True)
        d_scores = (probs_again * (d_probs - row_inner)).astype(jnp.bfloat16)
        d_query_block = (
            jnp.einsum(
                "hqk,kd->qhd", d_scores, near_keyval[:, :HD], preferred_element_type=jnp.float32
            )
            * scale_factor
        )
        d_keys = (
            jnp.einsum("hqk,qhd->kd", d_scores, query_block, preferred_element_type=jnp.float32)
            * scale_factor
        )
        d_values = jnp.einsum(
            "hqk,qhd->kd",
            probs_again.astype(jnp.bfloat16),
            d_mixed_low,
            preferred_element_type=jnp.float32,
        )
        updated = carry + jnp.concatenate([d_keys, d_values], axis=1)
        return (updated, d_query_block)

    d_keyval, d_query_blocks = lax.scan(
        backward_block,
        jnp.zeros((tokens + tokens, 2 * HD), jnp.float32),
        (block_starts, log_blocks),
    )
    d_queries = d_query_blocks.reshape(tokens, local_heads, HD)
    returned = from_behind(d_keyval[:tokens].astype(jnp.bfloat16), "context", -1).astype(
        jnp.float32
    )
    own_grad = d_keyval[tokens:].at[keep_from:].add(returned)
    d_query_raw, gain_query = query_back(d_queries)
    d_query_low = d_query_raw.reshape(tokens, local_heads * HD).astype(jnp.bfloat16)
    d_normed_query, keyval_grad, gain_query_all = (
        lax.psum(contract_last(d_query_low, query_all).astype(jnp.bfloat16), "tensor").astype(
            jnp.float32
        ),
        lax.psum(own_grad.astype(jnp.bfloat16), "tensor").astype(jnp.float32),
        lax.psum(gain_query.astype(jnp.bfloat16), "tensor").astype(jnp.float32),
    )
    d_key_raw, gain_key = key_back(keyval_grad[:, None, :HD])
    d_keyval_low = jnp.concatenate([d_key_raw[:, 0], keyval_grad[:, HD:]], axis=1).astype(
        jnp.bfloat16
    )
    d_normed = d_normed_query + contract_last(d_keyval_low, keyval_all)
    d_input_norm, gain_input = input_back(d_normed)
    input_total = d_hidden + d_input_norm
    features = normed
    grad_cols = branch_low
    attn_grads = lax.psum_scatter(
        jnp.stack(
            [contract_first(features, d_query_low), contract_first(grad_cols, mixed_low)], axis=1
        ).astype(jnp.bfloat16),
        ("fsdp", "context"),
        scatter_dimension=0,
        tiled=True,
    ).astype(jnp.float32)
    keyval_term = contract_first(normed, d_keyval_low)
    gain_terms = jnp.stack([gain_input, gain_post_attn, gain_pre_mlp, gain_post_mlp])
    head_terms = jnp.stack([gain_query_all, gain_key])
    gain_grad, head_grad, keyval_weight_grad = (
        lax.psum_scatter(
            gain_terms.astype(jnp.bfloat16), ("fsdp", "context"), scatter_dimension=1, tiled=True
        ).astype(jnp.float32),
        lax.psum_scatter(
            head_terms.astype(jnp.bfloat16), ("fsdp", "context"), scatter_dimension=1, tiled=True
        ).astype(jnp.float32),
        lax.psum_scatter(
            keyval_term.astype(jnp.bfloat16), ("fsdp", "context"), scatter_dimension=0, tiled=True
        ).astype(jnp.float32),
    )
    return (
        result[None].astype(jnp.bfloat16),
        input_total[None].astype(jnp.bfloat16),
        gain_grad,
        head_grad,
        attn_grads[:, 0],
        keyval_weight_grad,
        attn_grads[:, 1],
        jnp.stack([gate_grad, up_grad], axis=1),
        down_grad,
    )


def solution(mesh):
    return jax.shard_map(
        shards,
        mesh=mesh,
        in_specs=(
            P("fsdp", "context", None),
            P("fsdp", "context"),
            P("fsdp", "context"),
            P(None, ("fsdp", "context")),
            P(None, ("fsdp", "context")),
            P(("fsdp", "context"), "tensor"),
            P(("fsdp", "context"), None),
            P(("fsdp", "context"), "tensor"),
            P(("fsdp", "context"), None, "tensor"),
            P(("fsdp", "context"), "tensor"),
            P("fsdp", "context", None),
        ),
        out_specs=(
            P("fsdp", "context", None),
            P("fsdp", "context", None),
            P(None, ("fsdp", "context")),
            P(None, ("fsdp", "context")),
            P(("fsdp", "context"), "tensor"),
            P(("fsdp", "context"), None),
            P(("fsdp", "context"), "tensor"),
            P(("fsdp", "context"), None, "tensor"),
            P(("fsdp", "context"), "tensor"),
        ),
        check_vma=False,
    )
```

profile of v0, /device:TPU:0, one launch (start us, length us, event | category | flops | bytes accessed | tf_op | source)
XLA Modules:
  0.0 1111.7 jit_solution(1959116816128827641)
XLA Ops:
  8.7 4.9 collective-permute-start.1
  14.3 18.8 %all-gather.1 = bf16[8,32,2]{1,2,0:T(2,128)(2,1)S(1)} all-gather(bf16[1,32,2]{1,2,0:T(2,128)(2,1)} %bitcast.266), channel_id=1, replica_groups=mesh['fsdp'=2,'context'=4,'tensor'=4] {'fsdp','context'}, dimensions={0}, use_global_device_ids=true | all-gather | bytes 1152 | tf_op jit(solution)/shard_map/all_gather | solution.py:73
  33.2 27.2 %all-gather = bf16[8,144,4]{1,2,0:T(4,128)(2,1)S(1)} all-gather(bf16[1,144,4]{1,2,0:T(4,128)(2,1)} %bitcast.265), channel_id=1, replica_groups=mesh['fsdp'=2,'context'=4,'tensor'=4] {'fsdp','context'}, dimensions={0}, use_global_device_ids=true | all-gather | bytes 10368 | tf_op jit(solution)/shard_map/all_gather | solution.py:72
  62.8 32.5 %all_gather.26 = bf16[1152,256]{1,0:T(8,128)(2,1)S(1)} all-gather(bf16[144,256]{1,0:T(8,128)(2,1)} %param.20), channel_id=1, replica_groups=mesh['fsdp'=2,'context'=4,'tensor'=4] {'fsdp','context'}, dimensions={0}, use_global_device_ids=true | all-gather | bytes 663552 | tf_op jit(solution)/shard_map/all_gather | solution.py:74
  96.1 2.0 multiply_reduce_fusion.1
  99.1 2.2 fusion.131
  104.4 33.8 %all_gather.27 = bf16[1152,256]{1,0:T(8,128)(2,1)S(1)} all-gather(bf16[144,256]{1,0:T(8,128)(2,1)S(1)} %copy-done.32), channel_id=1, replica_groups=mesh['fsdp'=2,'context'=4,'tensor'=4] {'fsdp','context'}, dimensions={0}, use_global_device_ids=true | all-gather | bytes 663552 | tf_op jit(solution)/shard_map/all_gather | solution.py:76
  138.4 2.0 fusion.140
  143.1 2.3 copy.32
  146.2 36.1 %all-reduce.13.cloned.1.call-done = bf16[512,1152]{1,0:T(8,128)(2,1)} async-done(((bf16[512,1152]{1,0:T(8,128)(2,1)}), bf16[512,1152]{1,0:T(8,128)(2,1)}) %all-reduce.13.cloned.1.call-update) | async-done | bytes 1179664 | tf_op jit(solution)/shard_map/psum | solution.py:136
  185.1 2.3 multiply_reduce_fusion
  188.6 119.4 %all-gather.8.cloned.1.call-done = bf16[1152,2,1728]{2,0,1:T(8,128)(2,1)} async-done(((bf16[144,2,1728]{2,0,1:T(8,128)(2,1)}), bf16[1152,2,1728]{2,0,1:T(8,128)(2,1)}) %all-gather.8.cloned.1.call-update) | async-done | bytes 7962640 | tf_op jit(solution)/shard_map/all_gather | solution.py:147
  308.0 8.2 fusion.114
  316.2 2.9 copy-done.8
  319.1 2.4 multiply_convert_fusion
  321.5 58.5 %all-gather.10.cloned.1.call-done = bf16[1152,1728]{1,0:T(8,128)(2,1)} async-done(((bf16[144,1728]{1,0:T(8,128)(2,1)}), bf16[1152,1728]{1,0:T(8,128)(2,1)}) %all-gather.10.cloned.1.call-update) | async-done | bytes 3981328 | tf_op jit(solution)/shard_map/all_gather | solution.py:154
  380.0 6.3 convolution_convert_fusion.4
  386.6 36.0 %all-reduce.15.cloned.1.call-done = bf16[512,1152]{1,0:T(8,128)(2,1)} async-done(((bf16[512,1152]{1,0:T(8,128)(2,1)}), bf16[512,1152]{1,0:T(8,128)(2,1)}) %all-reduce.15.cloned.1.call-update) | async-done | bytes 1179664 | tf_op jit(solution)/shard_map/psum | solution.py:152
  424.4 3.4 fusion.38
  427.9 10.7 multiply_bitcast_fusion
  440.3 8.1 fusion.7
  450.2 36.1 %all-reduce.17.cloned.1.call-done = bf16[512,1152]{1,0:T(8,128)(2,1)} async-done(((bf16[512,1152]{1,0:T(8,128)(2,1)}), bf16[512,1152]{1,0:T(8,128)(2,1)}) %all-reduce.17.cloned.1.call-update) | async-done | bytes 1179664 | tf_op jit(solution)/shard_map/psum | solution.py:176
  486.4 3.6 fusion.29
  490.1 5.1 fusion.25
  505.7 11.6 %collective-permute-done.2 = bf16[512,512]{0,1:T(8,128)(2,1)S(1)} collective-permute-done((bf16[512,512]{0,1:T(8,128)(2,1)S(1)}, bf16[512,512]{0,1:T(8,128)(2,1)S(1)}, u32[]{:S(2)}, u32[]{:S(2)}) %collective-permute-start.2) | collective-permute-done | bytes 524320 | tf_op jit(solution)/shard_map/ppermute | solution.py:14
  523.5 7.2 psum.47
  530.7 2.3 fusion.22
  533.0 2.5 fusion.21
  535.6 27.2 %all-reduce.19.cloned.1.call-done = (bf16[512,1152]{1,0:T(8,128)(2,1)}, bf16[512,512]{0,1:T(8,128)(2,1)}) async-done(((bf16[512,1152]{1,0:T(8,128)(2,1)}, bf16[512,512]{0,1:T(8,128)(2,1)}), (bf16[512,1152]{1,0:T(8,128)(2,1)}, bf16[512,512]{0,1:T(8,128)(2,1)})) %all-reduce.19.cloned.1.call-update) | async-done | bytes 1703952 | tf_op jit(solution)/shard_map/psum | solution.py:237
  565.7 3.2 fusion.27
  576.1 3.1 convolution_convert_fusion.2
  579.3 9.3 convolution_convert_fusion
  588.6 3.5 slice_bitcast_fusion.1
  592.1 6.5 copy.38
  598.6 6.5 copy.40
  606.8 6.3 convolution_convert_fusion.1
  613.8 4.0 fusion.52
  617.8 16.4 %reduce-scatter.24.cloned.1.call-done = bf16[32,2]{1,0:T(8,128)(2,1)} async-done(((bf16[256,2]{1,0:T(8,128)(2,1)}), bf16[32,2]{1,0:T(8,128)(2,1)}) %reduce-scatter.24.cloned.1.call-update) | async-done | bytes 144
  635.6 60.7 %reduce-scatter.22.cloned.1.call-done = bf16[144,4]{1,0:T(8,128)(2,1)} async-done(((bf16[1152,4]{1,0:T(8,128)(2,1)}), bf16[144,4]{1,0:T(8,128)(2,1)}) %reduce-scatter.22.cloned.1.call-update) | async-done | bytes 1168
  697.8 65.6 %reduce-scatter.16.cloned.1.call-done = bf16[144,2,256]{2,0,1:T(8,128)(2,1)} async-done(((bf16[1152,2,256]{2,0,1:T(8,128)(2,1)}), bf16[144,2,256]{2,0,1:T(8,128)(2,1)}) %reduce-scatter.16.cloned.1.call-update) | async-done | bytes 147472 | tf_op jit(solution)/shard_map/reduce_scatter | solution.py:252
  765.0 65.4 %reduce-scatter.18.cloned.1.call-done = bf16[144,512]{1,0:T(8,128)(2,1)} async-done(((bf16[1152,512]{1,0:T(8,128)(2,1)}), bf16[144,512]{1,0:T(8,128)(2,1)}) %reduce-scatter.18.cloned.1.call-update) | async-done | bytes 147472 | tf_op jit(solution)/shard_map/reduce_scatter | solution.py:270
  832.1 88.7 %reduce-scatter.26.cloned.1.call-done = bf16[144,1728]{1,0:T(8,128)(2,1)} async-done(((bf16[1152,1728]{1,0:T(8,128)(2,1)}), bf16[144,1728]{1,0:T(8,128)(2,1)}) %reduce-scatter.26.cloned.1.call-update) | async-done | bytes 497680
  920.8 2.3 copy.39
  923.1 88.9 %reduce-scatter.28.cloned.1.call-done = bf16[144,1728]{1,0:T(8,128)(2,1)} async-done(((bf16[1152,1728]{1,0:T(8,128)(2,1)}), bf16[144,1728]{1,0:T(8,128)(2,1)}) %reduce-scatter.28.cloned.1.call-update) | async-done | bytes 497680
  1011.9 2.3 copy.41
  1016.1 3.2 copy.33
  1019.2 83.7 %reduce-scatter.20.cloned.1.call-done = bf16[144,1728]{1,0:T(8,128)(2,1)} async-done(((bf16[1152,1728]{1,0:T(8,128)(2,1)}), bf16[144,1728]{1,0:T(8,128)(2,1)}) %reduce-scatter.20.cloned.1.call-update) | async-done | bytes 497680 | tf_op jit(solution)/shard_map/reduce_scatter | solution.py:185
  1102.9 2.1 convert_element_type.221
  (279 shorter events, 59.2 us)
Async XLA Ops:
  7.2 91.9 %all-gather.6.cloned.1.call-start = ((), (), s32[]{:S(2)}) async-start(), calls=%async_computation.7 | async-start | bytes 1327104 | tf_op jit(solution)/shard_map/all_gather | solution.py:75
  7.9 174.4 %all-reduce.13.cloned.1.call-start = ((), (), s32[]{:S(2)}) async-start(), calls=%async_computation.8 | async-start | bytes 2359296 | tf_op jit(solution)/shard_map/psum | solution.py:136
  8.7 129.6 %collective-permute-start.1 = (s32[2,512]{1,0:T(2,128)S(1)}, s32[2,512]{1,0:T(2,128)S(1)}, u32[]{:S(2)}, u32[]{:S(2)}) collective-permute-start(s32[2,512]{1,0:T(2,128)S(1)} %pad_add_fusion.2), channel_id=1, source_target_pairs={{0,4},{4,8},{8,12},{1,5},{5,9},{9,13},{2,6},{6,10},{10,14},{3,7},{... | collective-permute-start | bytes 12296 | tf_op jit(solution)/shard_map/ppermute | solution.py:14
  14.3 87.4 %copy-start.37 = (f32[512]{0:T(512)}, f32[512]{0:T(512)S(1)}, u32[]{:S(2)}) copy-start(f32[512]{0:T(512)S(1)} %convert_element_type.178) | copy-start | bytes 6148
  60.5 41.2 %copy-start.73 = (f32[128]{0:T(128)}, f32[128]{0:T(128)S(1)}, u32[]{:S(2)}) copy-start(f32[128]{0:T(128)S(1)} %multiply_power_fusion) | copy-start | bytes 1540
  61.1 38.0 %copy-start.44 = (f32[1152]{0:T(1024)}, f32[1152]{0:T(1024)S(1)}, u32[]{:S(2)}) copy-start(f32[1152]{0:T(1024)S(1)} %get-tuple-element.146) | copy-start | bytes 13828
  62.7 36.3 %copy-start.52 = (f32[512]{0:T(512)}, f32[512]{0:T(512)S(1)}, u32[]{:S(2)}) copy-start(f32[512]{0:T(512)S(1)} %fusion.30) | copy-start | bytes 6148
  62.7 36.4 %copy-start.70 = (f32[512]{0:T(512)}, f32[512]{0:T(512)S(1)}, u32[]{:S(2)}) copy-start(f32[512]{0:T(512)S(1)} %fusion.116) | copy-start | bytes 6148
  62.7 36.3 %copy-start.63 = (f32[1,256]{1,0:T(1,128)}, f32[1,256]{1,0:T(1,128)S(1)}, u32[]{:S(2)}) copy-start(f32[1,256]{1,0:T(1,128)S(1)} %get-tuple-element.171) | copy-start | bytes 3076
  62.8 38.8 %copy-start.61 = (f32[1,256]{1,0:T(1,128)}, f32[1,256]{1,0:T(1,128)S(1)}, u32[]{:S(2)}) copy-start(f32[1,256]{1,0:T(1,128)S(1)} %get-tuple-element.172) | copy-start | bytes 3076
  62.8 36.3 %copy-start.1 = (bf16[1,512,1152]{2,1,0:T(8,128)(2,1)S(1)}, bf16[1,512,1152]{2,1,0:T(8,128)(2,1)}, u32[]{:S(2)}) copy-start(bf16[1,512,1152]{2,1,0:T(8,128)(2,1)} %param.15) | copy-start | bytes 3538948
  101.5 36.7 %copy-start.60 = (s32[1,512]{1,0:T(1,128)S(1)}, s32[1,512]{1,0:T(1,128)}, u32[]{:S(2)}) copy-start(s32[1,512]{1,0:T(1,128)} %param.16) | copy-start | bytes 6148
  101.6 36.7 %copy-start.67 = (s32[1,512]{1,0:T(1,128)S(1)}, s32[1,512]{1,0:T(1,128)}, u32[]{:S(2)}) copy-start(s32[1,512]{1,0:T(1,128)} %param.17) | copy-start | bytes 6148
  103.0 35.3 %collective-permute-start = (bf16[512,512]{0,1:T(8,128)(2,1)S(1)}, bf16[512,512]{0,1:T(8,128)(2,1)S(1)}, u32[]{:S(2)}, u32[]{:S(2)}) collective-permute-start(bf16[512,512]{0,1:T(8,128)(2,1)S(1)} %pad_maximum_fusion.2), channel_id=1, source_target_pairs={{0,4},{4,8},{8,12},{1,5},{5,9},{9,13},{2,6},{6,10},{10,14},{3,7},{... | collective-permute-start | bytes 1572872 | tf_op jit(solution)/shard_map/ppermute | solution.py:14
  141.4 3.9 copy-start.26
  143.0 165.0 %all-gather.8.cloned.1.call-start = ((), (), s32[]{:S(2)}) async-start(), calls=%async_computation.9 | async-start | bytes 9289728 | tf_op jit(solution)/shard_map/all_gather | solution.py:147
  145.4 234.7 %all-gather.10.cloned.1.call-start = ((), (), s32[]{:S(2)}) async-start(), calls=%async_computation.10 | async-start | bytes 4644864 | tf_op jit(solution)/shard_map/all_gather | solution.py:154
  145.9 276.7 %all-reduce.15.cloned.1.call-start = ((), (), s32[]{:S(2)}) async-start(), calls=%async_computation.11 | async-start | bytes 2359296 | tf_op jit(solution)/shard_map/psum | solution.py:152
  182.3 125.7 %copy-start = (bf16[512,1152]{1,0:T(8,128)(2,1)S(1)}, bf16[512,1152]{1,0:T(8,128)(2,1)}, u32[]{:S(2)}) copy-start(bf16[512,1152]{1,0:T(8,128)(2,1)} %all-reduce.13.cloned.1.call-done) | copy-start | bytes 3538948
  386.4 100.0 %all-reduce.17.cloned.1.call-start = ((), (), s32[]{:S(2)}) async-start(), calls=%async_computation.12 | async-start | bytes 2359296 | tf_op jit(solution)/shard_map/psum | solution.py:176
  422.7 5.2 copy-start.5
  422.7 5.2 copy-start.12
  424.4 14.2 %copy-start.47 = (f32[512]{0:T(512)}, f32[512]{0:T(512)S(1)}, u32[]{:S(2)}) copy-start(f32[512]{0:T(512)S(1)} %fusion.121) | copy-start | bytes 6148
  424.4 15.9 %slice-start = ((s8[8257536]{0:T(1024)(128)(4,1)}), s8[4194304]{0:T(1024)(128)(4,1)S(1)}, s32[]{:S(2)}) async-start(s8[8257536]{0:T(1024)(128)(4,1)} %bitcast.267), calls=%async_computation.21 | async-start | bytes 8388608
  427.8 10.7 copy-start.77
  427.9 12.5 %slice-start.1 = ((s8[8257536]{0:T(1024)(128)(4,1)}), s8[4063232]{0:T(1024)(128)(4,1)S(1)}, s32[]{:S(2)}) async-start(s8[8257536]{0:T(1024)(128)(4,1)} %bitcast.267), calls=%async_computation.22 | async-start | bytes 8126464
  448.5 114.3 %all-reduce.19.cloned.1.call-start = ((), (), s32[]{:S(2)}) async-start(), calls=%async_computation.20 | async-start | bytes 3407872 | tf_op jit(solution)/shard_map/psum | solution.py:237
  490.1 5.1 copy-start.57
  501.8 15.5 %collective-permute-start.2 = (bf16[512,512]{0,1:T(8,128)(2,1)S(1)}, bf16[512,512]{0,1:T(8,128)(2,1)S(1)}, u32[]{:S(2)}, u32[]{:S(2)}) collective-permute-start(bf16[512,512]{0,1:T(8,128)(2,1)S(1)} %fusion.66), channel_id=1, source_target_pairs={{4,0},{8,4},{12,8},{5,1},{9,5},{13,9},{6,2},{10,6},{14,10},{7,3},{... | collective-permute-start | bytes 1572872 | tf_op jit(solution)/shard_map/ppermute | solution.py:14
  504.1 13.2 %copy-start.25 = (bf16[512,256]{0,1:T(8,128)(2,1)}, bf16[512,256]{0,1:T(8,128)(2,1)S(1)}, u32[]{:S(2)}) copy-start(bf16[512,256]{0,1:T(8,128)(2,1)S(1)} %fusion.108) | copy-start | bytes 786436
  505.7 25.0 %copy-start.17 = (bf16[512,1152]{1,0:T(8,128)(2,1)S(1)}, bf16[512,1152]{1,0:T(8,128)(2,1)}, u32[]{:S(2)}) copy-start(bf16[512,1152]{1,0:T(8,128)(2,1)} %copy-done.16) | copy-start | bytes 3538948
  518.3 14.7 %copy-start.3 = (bf16[1,512,1152]{2,1,0:T(8,128)(2,1)S(1)}, bf16[1,512,1152]{2,1,0:T(8,128)(2,1)}, u32[]{:S(2)}) copy-start(bf16[1,512,1152]{2,1,0:T(8,128)(2,1)} %param.15) | copy-start | bytes 3538948
  518.3 115.9 %reduce-scatter.24.cloned.1.call-start = ((), (), s32[]{:S(2)}) async-start(), calls=%async_computation.17 | async-start | bytes 73728
  533.0 31.0 %copy-start.39 = (f32[512]{0:T(512)S(1)}, f32[512]{0:T(512)}, u32[]{:S(2)}) copy-start(f32[512]{0:T(512)} %copy-done.37) | copy-start | bytes 6148
  533.0 31.0 %copy-start.75 = (f32[128]{0:T(128)S(1)}, f32[128]{0:T(128)}, u32[]{:S(2)}) copy-start(f32[128]{0:T(128)} %copy-done.73) | copy-start | bytes 1540
  533.0 32.2 %copy-start.10 = (f32[512,512]{0,1:T(8,128)S(1)}, f32[512,512]{0,1:T(8,128)}, u32[]{:S(2)}) copy-start(f32[512,512]{0,1:T(8,128)} %copy-done.9) | copy-start | bytes 3145732
  533.0 32.2 %copy-start.41 = (f32[512]{0:T(512)S(1)}, f32[512]{0:T(512)}, u32[]{:S(2)}) copy-start(f32[512]{0:T(512)} %copy-done.40) | copy-start | bytes 6148
  533.0 32.2 %copy-start.62 = (f32[1,256]{1,0:T(1,128)S(1)}, f32[1,256]{1,0:T(1,128)}, u32[]{:S(2)}) copy-start(f32[1,256]{1,0:T(1,128)} %copy-done.61) | copy-start | bytes 3076
  535.6 29.9 %copy-start.55 = (f32[512]{0:T(512)S(1)}, f32[512]{0:T(512)}, u32[]{:S(2)}) copy-start(f32[512]{0:T(512)} %copy-done.54) | copy-start | bytes 6148
  564.0 4.9 copy-start.28
  565.7 9.0 copy-start.22
  565.7 9.0 copy-start.27
  571.6 124.7 %reduce-scatter.22.cloned.1.call-start = ((), (), s32[]{:S(2)}) async-start(), calls=%async_computation.16 | async-start | bytes 331776
  574.6 188.8 %reduce-scatter.16.cloned.1.call-start = ((), (), s32[]{:S(2)}) async-start(), calls=%async_computation.13 | async-start | bytes 1327104 | tf_op jit(solution)/shard_map/reduce_scatter | solution.py:252
  575.9 254.5 %reduce-scatter.18.cloned.1.call-start = ((), (), s32[]{:S(2)}) async-start(), calls=%async_computation.14 | async-start | bytes 1327104 | tf_op jit(solution)/shard_map/reduce_scatter | solution.py:270
  579.2 341.6 %reduce-scatter.26.cloned.1.call-start = ((), (), s32[]{:S(2)}) async-start(), calls=%async_computation.18 | async-start | bytes 4644864
  598.6 413.3 %reduce-scatter.28.cloned.1.call-start = ((), (), s32[]{:S(2)}) async-start(), calls=%async_computation.19 | async-start | bytes 4644864
  605.2 497.7 %reduce-scatter.20.cloned.1.call-start = ((), (), s32[]{:S(2)}) async-start(), calls=%async_computation.15 | async-start | bytes 4644864 | tf_op jit(solution)/shard_map/reduce_scatter | solution.py:185
  (54 other events, 118.5 us)
Sparse Core Ops, SparseCore 0:
  10.1 43.7 all-gather.5
  143.1 39.0 all-reduce.12
  185.0 122.9 all-gather.7
  310.0 70.0 all-gather.9
  386.5 36.1 all-reduce.14
  448.6 37.7 all-reduce.16
  518.4 44.2 all-reduce.18
  571.7 62.4 reduce-scatter.23
  638.1 58.1 reduce-scatter.21
  699.5 63.8 reduce-scatter.15
  766.8 63.5 reduce-scatter.17
  833.8 86.9 reduce-scatter.25
  924.4 87.5 reduce-scatter.27
  1015.3 87.5 reduce-scatter.19
where the time goes:
time: 1120 us; the launch traced here: 1110 us
  waiting for transfers between devices  796 us (71%)
  blocking collectives  120 us (11%)
  matrix products  72.4 us (6%)
  local copies, waits for them, and re-layouts  50.5 us (5%)
  other arithmetic  49.1 us (4%)
  between operations  15.3 us (1%)
    unnamed x18, waiting for transfers between devices  256 us
    all_gather x1, waiting for transfers between devices, shards(): lax.all_gather(w_gateup, ('fsdp', 'context'), axis=0, tiled=True)  119 us
    reduce_scatter x1, waiting for transfers between devices, shards(): lax.psum_scatter(part.astype(jnp.bfloat16), ('fsdp', 'context'), scatter_...  83.7 us
    reduce_scatter x1, waiting for transfers between devices, shards(): lax.psum_scatter(jnp.stack([contract_first(features, d_query_low), contra...  65.6 us
    reduce_scatter x1, waiting for transfers between devices, shards(): lax.psum_scatter(keyval_term.astype(jnp.bfloat16), ('fsdp', 'context'), s...  65.4 us
    all_gather x1, waiting for transfers between devices, shards(): lax.all_gather(w_down, ('fsdp', 'context'), axis=0, tiled=True)  58.5 us
    unnamed x180, local copies, waits for them, and re-layouts  39.6 us
    psum x1, waiting for transfers between devices, shards(): lax.psum(d_normed_part.astype(jnp.bfloat16), 'tensor').astype(jnp.float32)  36.1 us
  transfers between devices with their start and end apart: 17, of which 14 were waited for; matrix products, arithmetic and copies ran while one was open for 9% of the time, Pallas kernels for 0%

commit v1 on v0

--- a/solution.py
+++ b/solution.py
@@ -141,12 +141,42 @@
     normed_mlp_f, pre_mlp_back = jax.vjp(rms_norm, hidden, gains_f[2])
     normed_mlp = normed_mlp_f.astype(jnp.bfloat16)
     columns = normed_mlp
-    gate_up = jnp.einsum(
+    size, index, rows = (
+        lax.axis_size(("fsdp", "context")),
+        lax.axis_index(("fsdp", "context")),
+        w_gateup.shape[0],
+    )
+    right = [(i_2, (i_2 + 1) % size) for i_2 in range(size)]
+    backward = [(i_2, (i_2 - 1) % size) for i_2 in range(size)]
+    half = size // 2
+    from_left = from_right = w_gateup
+    so_far = jnp.einsum(
         "bn,nkf->bkf",
-        columns,
-        lax.all_gather(w_gateup, ("fsdp", "context"), axis=0, tiled=True),
+        lax.dynamic_slice_in_dim(columns, index * rows, w_gateup.shape[0], axis=1),
+        w_gateup,
         preferred_element_type=jnp.float32,
     )
+    for lap in range(1, half + 1):
+        from_left = lax.ppermute(from_left, ("fsdp", "context"), right)
+        if lap < size - half:
+            from_right = lax.ppermute(from_right, ("fsdp", "context"), backward)
+            so_far = so_far + jnp.einsum(
+                "bn,nkf->bkf",
+                lax.dynamic_slice_in_dim(
+                    columns, (index + lap) % size * rows, from_right.shape[0], axis=1
+                ),
+                from_right,
+                preferred_element_type=jnp.float32,
+            )
+        so_far = so_far + jnp.einsum(
+            "bn,nkf->bkf",
+            lax.dynamic_slice_in_dim(
+                columns, (index - lap) % size * rows, from_left.shape[0], axis=1
+            ),
+            from_left,
+            preferred_element_type=jnp.float32,
+        )
+    gate_up = so_far
     active_f, glu_back = jax.vjp(glu, gate_up)
     active = active_f.astype(jnp.bfloat16)
     down = lax.psum(

time: 1120 us -> 1190 us (1.062)
  blocking collectives: 120 us -> 182 us
  matrix products: 72.4 us -> 126 us
  waiting for transfers between devices: 796 us -> 746 us
  starting transfers between devices: 9.23 us -> 23.6 us
    all_gather x1, waiting for transfers between devices: 58.5 us -> 6.79 us  [shards(): lax.all_gather(w_down, ('fsdp', 'context'), axis=0, tiled=True)]
    all_gather x1, blocking collectives: 27.2 us -> 76.2 us  [shards(): lax.all_gather(norm_gains, ('fsdp', 'context'), axis=1, tiled=True)]
    dot_general x1 -> x8, matrix products: 8.16 us -> 57 us  [the longest x4 36.6 us: shards(): jnp.einsum('bn,nkf->bkf', lax.dynamic_slice_in_dim(columns, (index - lap)...]
    unnamed x18, waiting for transfers between devices: 256 us -> 289 us
    ppermute x0 -> x7, waiting for transfers between devices: none -> 32.5 us  [the longest x3 32.5 us: shards(): from_right = lax.ppermute(from_right, ('fsdp', 'context'), backward)]
    psum x1, waiting for transfers between devices: 27.2 us -> 7.78 us  [shards(): lax.psum(contract_last(d_query_low, query_all).astype(jnp.bfloat16), 'ten...]
    psum x1, waiting for transfers between devices: 36.1 us -> 18.7 us  [shards(): lax.psum(contract_last(mixed_low, out_all).astype(jnp.bfloat16), 'tensor')]
    ppermute x0 -> x7, starting transfers between devices: none -> 16.1 us  [the longest x3 9.85 us: shards(): from_right = lax.ppermute(from_right, ('fsdp', 'context'), backward)]
  transfers between devices with their start and end apart: 17 -> 24, of which waited for: 14 -> 15; matrix products, arithmetic and copies ran while one was open for 9% -> 15% of each run, Pallas kernels for 0% -> 0%
where the time goes in v1:
time: 1190 us
  waiting for transfers between devices  746 us (63%)
  blocking collectives  182 us (15%)
  matrix products  126 us (11%)
  other arithmetic  51 us (4%)
  local copies, waits for them, and re-layouts  41.7 us (4%)
  starting transfers between devices  23.6 us (2%)
  between operations  15.4 us (1%)
    unnamed x18, waiting for transfers between devices  289 us
    all_gather x1, waiting for transfers between devices, shards(): lax.all_gather(w_gateup, ('fsdp', 'context'), axis=0, tiled=True)  108 us
    reduce_scatter x1, waiting for transfers between devices, shards(): lax.psum_scatter(part.astype(jnp.bfloat16), ('fsdp', 'context'), scatter_...  82 us
    all_gather x1, blocking collectives, shards(): lax.all_gather(norm_gains, ('fsdp', 'context'), axis=1, tiled=True)  76.2 us
    reduce_scatter x1, waiting for transfers between devices, shards(): lax.psum_scatter(jnp.stack([contract_first(features, d_query_low), contra...  65.8 us
    reduce_scatter x1, waiting for transfers between devices, shards(): lax.psum_scatter(keyval_term.astype(jnp.bfloat16), ('fsdp', 'context'), s...  65.2 us
    all_gather x1, blocking collectives, shards(): lax.all_gather(w_out, ('fsdp', 'context'), axis=0, tiled=True)  48.1 us
    dot_general x4, matrix products, shards(): jnp.einsum('bn,nkf->bkf', lax.dynamic_slice_in_dim(columns, (index - lap)...  36.6 us
  transfers between devices with their start and end apart: 24, of which 15 were waited for; matrix products, arithmetic and copies ran while one was open for 15% of the time, Pallas kernels for 0%

profile of v1, /device:TPU:0, one launch (start us, length us, event | category | flops | bytes accessed | tf_op | source)
XLA Modules:
  0.0 1185.0 jit_solution(4331570488017971483)
XLA Ops:
  8.7 6.1 collective-permute-start.2
  18.0 76.2 %all-gather = bf16[8,144,4]{1,2,0:T(4,128)(2,1)S(1)} all-gather(bf16[1,144,4]{1,2,0:T(4,128)(2,1)} %bitcast.290), channel_id=1, replica_groups=mesh['fsdp'=2,'context'=4,'tensor'=4] {'fsdp','context'}, dimensions={0}, use_global_device_ids=true | all-gather | bytes 10368 | tf_op jit(solution)/shard_map/all_gather | solution.py:72
  94.3 18.4 %all-gather.1 = bf16[8,32,2]{1,2,0:T(2,128)(2,1)S(1)} all-gather(bf16[1,32,2]{1,2,0:T(2,128)(2,1)} %bitcast.291), channel_id=1, replica_groups=mesh['fsdp'=2,'context'=4,'tensor'=4] {'fsdp','context'}, dimensions={0}, use_global_device_ids=true | all-gather | bytes 1152 | tf_op jit(solution)/shard_map/all_gather | solution.py:73
  114.3 32.9 %all_gather.25 = bf16[1152,256]{1,0:T(8,128)(2,1)S(1)} all-gather(bf16[144,256]{1,0:T(8,128)(2,1)S(1)} %copy-done.40), channel_id=1, replica_groups=mesh['fsdp'=2,'context'=4,'tensor'=4] {'fsdp','context'}, dimensions={0}, use_global_device_ids=true | all-gather | bytes 663552 | tf_op jit(solution)/shard_map/all_gather | solution.py:74
  149.7 4.1 collective-permute-start.5
  159.2 2.8 collective-permute-start
  161.9 48.1 %all_gather.26 = bf16[1152,256]{1,0:T(8,128)(2,1)S(1)} all-gather(bf16[144,256]{1,0:T(8,128)(2,1)S(1)} %copy-done.41), channel_id=1, replica_groups=mesh['fsdp'=2,'context'=4,'tensor'=4] {'fsdp','context'}, dimensions={0}, use_global_device_ids=true | all-gather | bytes 663552 | tf_op jit(solution)/shard_map/all_gather | solution.py:76
  211.5 3.8 collective-permute-start.4
  216.5 2.3 fusion.167
  223.4 32.5 %collective-permute-done.4 = bf16[144,2,1728]{2,0,1:T(8,128)(2,1)} collective-permute-done((bf16[144,2,1728]{2,0,1:T(8,128)(2,1)}, bf16[144,2,1728]{2,0,1:T(8,128)(2,1)}, u32[]{:S(2)}, u32[]{:S(2)}) %collective-permute-start.4) | collective-permute-done | bytes 995360 | tf_op jit(solution)/shard_map/ppermute | solution.py:162
  258.0 18.7 %all-reduce.13.cloned.1.call-done = bf16[512,1152]{1,0:T(8,128)(2,1)} async-done(((bf16[512,1152]{1,0:T(8,128)(2,1)}), bf16[512,1152]{1,0:T(8,128)(2,1)}) %all-reduce.13.cloned.1.call-update) | async-done | bytes 1179664 | tf_op jit(solution)/shard_map/psum | solution.py:136
  281.7 4.2 fusion.123
  285.9 5.4 fusion.115
  291.3 5.3 fusion.117
  296.6 5.3 fusion.119
  302.0 5.4 fusion.121
  307.3 5.3 fusion.111
  312.6 5.5 fusion.113
  318.1 20.6 %add_add_fusion = f32[512,2,1728]{0,2,1:T(8,128)} fusion(f32[512,2,1728]{0,2,1:T(8,128)} %fusion.111, f32[512,2,1728]{0,2,1:T(8,128)} %fusion.113, f32[512,2,1728]{0,2,1:T(8,128)} %fusion.115, f32[512,2,1728]{0,2,1:T(8,128)} %fusion.117, f32[512,2,1728]{0,2,1:T(8,128)} %fusion.119, f32[512,2,1728]{0,2,1:T(8,128)} %fusion.123, f32[512,2,1728]{0,2,1:T(8,128)} %fusion.121, ...), kind=kOutput, calls=%fused_computation.3 | convolution fusion | flops 521994240 | bytes 57880580 | tf_op jit(solution)/shard_map/bn,nkf->bkf/dot_general | solution.py:171
  338.7 5.5 multiply_convert_fusion
  344.2 6.8 all-gather.8.cloned.1.call-done
  351.0 6.3 convolution_convert_fusion.4
  358.6 35.0 %all-reduce.15.cloned.1.call-done = bf16[512,1152]{1,0:T(8,128)(2,1)} async-done(((bf16[512,1152]{1,0:T(8,128)(2,1)}), bf16[512,1152]{1,0:T(8,128)(2,1)}) %all-reduce.15.cloned.1.call-update) | async-done | bytes 1179664 | tf_op jit(solution)/shard_map/psum | solution.py:182
  395.3 3.2 fusion.38
  399.1 11.9 %multiply_bitcast_fusion = (f32[512,1,1728]{0,2,1:T(8,128)}, f32[512,1,1728]{0,2,1:T(8,128)}) fusion(f32[512,2,1728]{0,2,1:T(8,128)} %add_add_fusion, bf16[1152,1728]{1,0:T(8,128)(2,1)} %all-gather.8.cloned.1.call-done, bf16[512,1152]{1,0:T(8,128)(2,1)S(1)} %copy-done.6, bf16[1,512,1152]{2,1,0:T(8,128)(2,1)} %param.25, f32[512]{0:T(512)S(1)} %multiply_multiply_fusion.8, ...), kind=kOutput, calls=%fused_computation.25 | convolution fusion | flops 2062614528 | bytes 20505088 | tf_op jit(solution)/shard_map/dot_general | solution.py:194
  411.0 108.2 %all-gather.10.cloned.1.call-done = bf16[1152,2,1728]{2,0,1:T(8,128)(2,1)} async-done(((bf16[144,2,1728]{2,0,1:T(8,128)(2,1)}), bf16[1152,2,1728]{2,0,1:T(8,128)(2,1)}) %all-gather.10.cloned.1.call-update) | async-done | bytes 7962640 | tf_op jit(solution)/shard_map/all_gather | solution.py:203
  519.2 11.4 fusion.7
  531.1 11.4 convolution_convert_fusion
  542.6 23.9 %all-reduce.17.cloned.1.call-done = bf16[512,1152]{1,0:T(8,128)(2,1)} async-done(((bf16[512,1152]{1,0:T(8,128)(2,1)}), bf16[512,1152]{1,0:T(8,128)(2,1)}) %all-reduce.17.cloned.1.call-update) | async-done | bytes 1179664 | tf_op jit(solution)/shard_map/psum | solution.py:206
  566.5 3.3 fusion.29
  569.8 4.0 fusion.25
  585.2 10.2 collective-permute-done.9
  596.5 5.7 slice_bitcast_fusion.1
  602.2 6.5 copy.98
  608.8 6.5 copy.100
  616.5 6.3 convolution_convert_fusion.1
  623.6 6.4 psum.47
  633.1 7.8 all-reduce.19.cloned.1.call-done
  645.0 5.0 fusion.27
  654.7 77.6 %reduce-scatter.26.cloned.1.call-done = bf16[144,1728]{1,0:T(8,128)(2,1)} async-done(((bf16[1152,1728]{1,0:T(8,128)(2,1)}), bf16[144,1728]{1,0:T(8,128)(2,1)}) %reduce-scatter.26.cloned.1.call-update) | async-done | bytes 497680
  733.7 89.8 %reduce-scatter.28.cloned.1.call-done = bf16[144,1728]{1,0:T(8,128)(2,1)} async-done(((bf16[1152,1728]{1,0:T(8,128)(2,1)}), bf16[144,1728]{1,0:T(8,128)(2,1)}) %reduce-scatter.28.cloned.1.call-update) | async-done | bytes 497680
  827.0 5.4 copy.77
  832.4 82.0 %reduce-scatter.20.cloned.1.call-done = bf16[144,1728]{1,0:T(8,128)(2,1)} async-done(((bf16[1152,1728]{1,0:T(8,128)(2,1)}), bf16[144,1728]{1,0:T(8,128)(2,1)}) %reduce-scatter.20.cloned.1.call-update) | async-done | bytes 497680 | tf_op jit(solution)/shard_map/reduce_scatter | solution.py:215
  917.1 3.3 fusion.51
  920.5 60.0 %reduce-scatter.24.cloned.1.call-done = bf16[32,2]{1,0:T(8,128)(2,1)} async-done(((bf16[256,2]{1,0:T(8,128)(2,1)}), bf16[32,2]{1,0:T(8,128)(2,1)}) %reduce-scatter.24.cloned.1.call-update) | async-done | bytes 144
  981.8 60.6 %reduce-scatter.22.cloned.1.call-done = bf16[144,4]{1,0:T(8,128)(2,1)} async-done(((bf16[1152,4]{1,0:T(8,128)(2,1)}), bf16[144,4]{1,0:T(8,128)(2,1)}) %reduce-scatter.22.cloned.1.call-update) | async-done | bytes 1168
  1043.9 65.8 %reduce-scatter.16.cloned.1.call-done = bf16[144,2,256]{2,0,1:T(8,128)(2,1)} async-done(((bf16[1152,2,256]{2,0,1:T(8,128)(2,1)}), bf16[144,2,256]{2,0,1:T(8,128)(2,1)}) %reduce-scatter.16.cloned.1.call-update) | async-done | bytes 147472 | tf_op jit(solution)/shard_map/reduce_scatter | solution.py:282
  1111.4 65.2 %reduce-scatter.18.cloned.1.call-done = bf16[144,512]{1,0:T(8,128)(2,1)} async-done(((bf16[1152,512]{1,0:T(8,128)(2,1)}), bf16[144,512]{1,0:T(8,128)(2,1)}) %reduce-scatter.18.cloned.1.call-update) | async-done | bytes 147472 | tf_op jit(solution)/shard_map/reduce_scatter | solution.py:300
  (302 shorter events, 71.7 us)
Async XLA Ops:
  7.2 140.1 %copy-start.64 = (s32[1,512]{1,0:T(1,128)S(1)}, s32[1,512]{1,0:T(1,128)}, u32[]{:S(2)}) copy-start(s32[1,512]{1,0:T(1,128)} %param.16) | copy-start | bytes 6148
  7.2 106.2 %copy-start.1 = (bf16[1,512,1152]{2,1,0:T(8,128)(2,1)S(1)}, bf16[1,512,1152]{2,1,0:T(8,128)(2,1)}, u32[]{:S(2)}) copy-start(bf16[1,512,1152]{2,1,0:T(8,128)(2,1)} %param.15) | copy-start | bytes 3538948
  7.2 107.1 %copy-start.40 = (bf16[144,256]{1,0:T(8,128)(2,1)S(1)}, bf16[144,256]{1,0:T(8,128)(2,1)}, u32[]{:S(2)}) copy-start(bf16[144,256]{1,0:T(8,128)(2,1)} %param.20) | copy-start | bytes 221188
  7.2 146.6 %all-gather.6.cloned.1.call-start = ((), (), s32[]{:S(2)}) async-start(), calls=%async_computation.7 | async-start | bytes 1327104 | tf_op jit(solution)/shard_map/all_gather | solution.py:75
  8.7 139.3 %copy-start.18 = (bf16[144,2,1728]{2,0,1:T(8,128)(2,1)}, bf16[144,2,1728]{2,0,1:T(8,128)(2,1)S(1)}, u32[]{:S(2)}) copy-start(bf16[144,2,1728]{2,0,1:T(8,128)(2,1)S(1)} %copy.66) | copy-start | bytes 2985988
  8.7 202.9 %collective-permute-start.2 = (bf16[144,2,1728]{2,0,1:T(8,128)(2,1)S(1)}, bf16[144,2,1728]{2,0,1:T(8,128)(2,1)}, u32[]{:S(2)}, u32[]{:S(2)}) collective-permute-start(bf16[144,2,1728]{2,0,1:T(8,128)(2,1)S(1)} %copy.66), channel_id=1, source_target_pairs={{0,28},{4,0},{8,4},{12,8},{16,12},{20,16},{24,20},{28,24},{1,29},{... | collective-permute-start | bytes 2985992 | tf_op jit(solution)/shard_map/ppermute | solution.py:162
  14.7 135.0 %collective-permute-start.3 = (bf16[144,2,1728]{2,0,1:T(8,128)(2,1)S(1)}, bf16[144,2,1728]{2,0,1:T(8,128)(2,1)}, u32[]{:S(2)}, u32[]{:S(2)}) collective-permute-start(bf16[144,2,1728]{2,0,1:T(8,128)(2,1)S(1)} %copy.66), channel_id=1, source_target_pairs={{0,4},{4,8},{8,12},{12,16},{16,20},{20,24},{24,28},{28,0},{1,5},{5... | collective-permute-start | bytes 2985992 | tf_op jit(solution)/shard_map/ppermute | solution.py:160
  14.8 262.0 %all-reduce.13.cloned.1.call-start = ((), (), s32[]{:S(2)}) async-start(), calls=%async_computation.8 | async-start | bytes 2359296 | tf_op jit(solution)/shard_map/psum | solution.py:136
  16.1 193.9 %collective-permute-start.1 = (s32[2,512]{1,0:T(2,128)}, s32[2,512]{1,0:T(2,128)}, u32[]{:S(2)}, u32[]{:S(2)}) collective-permute-start(s32[2,512]{1,0:T(2,128)} %pad_add_fusion.2), channel_id=1, source_target_pairs={{0,4},{4,8},{8,12},{1,5},{5,9},{9,13},{2,6},{6,10},{10,14},{3,7},{... | collective-permute-start | bytes 12296 | tf_op jit(solution)/shard_map/ppermute | solution.py:14
  113.3 40.5 %copy-start.51 = (f32[1152]{0:T(1024)}, f32[1152]{0:T(1024)S(1)}, u32[]{:S(2)}) copy-start(f32[1152]{0:T(1024)S(1)} %get-tuple-element.146) | copy-start | bytes 13828
  114.2 39.6 %copy-start.79 = (f32[512]{0:T(512)}, f32[512]{0:T(512)S(1)}, u32[]{:S(2)}) copy-start(f32[512]{0:T(512)S(1)} %fusion.144) | copy-start | bytes 6148
  147.1 9.0 copy-start.19
  147.2 9.3 copy-start.81
  147.2 9.2 copy-start.43
  147.3 9.1 copy-start.69
  149.7 65.6 %collective-permute-start.5 = (bf16[144,2,1728]{2,0,1:T(8,128)(2,1)}, bf16[144,2,1728]{2,0,1:T(8,128)(2,1)}, u32[]{:S(2)}, u32[]{:S(2)}) collective-permute-start(bf16[144,2,1728]{2,0,1:T(8,128)(2,1)} %collective-permute-done.3), channel_id=1, source_target_pairs={{0,4},{4,8},{8,12},{12,16},{16,20},{20,24},{24,28},{28,0},{1,5},{5... | collective-permute-start | bytes 2985992 | tf_op jit(solution)/shard_map/ppermute | solution.py:160
  156.3 53.7 %copy-start.45 = (f32[512]{0:T(512)}, f32[512]{0:T(512)S(1)}, u32[]{:S(2)}) copy-start(f32[512]{0:T(512)S(1)} %fusion.145) | copy-start | bytes 6148
  158.3 60.5 %copy-start.30 = (bf16[512,128]{0,1:T(8,128)(2,1)}, bf16[512,128]{0,1:T(8,128)(2,1)S(1)}, u32[]{:S(2)}) copy-start(bf16[512,128]{0,1:T(8,128)(2,1)S(1)} %get-tuple-element.159) | copy-start | bytes 393220
  158.3 58.2 %copy-start.65 = (s32[1,512]{1,0:T(1,128)S(1)}, s32[1,512]{1,0:T(1,128)}, u32[]{:S(2)}) copy-start(s32[1,512]{1,0:T(1,128)} %param.16) | copy-start | bytes 6148
  159.2 56.1 %collective-permute-start = (bf16[512,512]{0,1:T(8,128)(2,1)}, bf16[512,512]{0,1:T(8,128)(2,1)}, u32[]{:S(2)}, u32[]{:S(2)}) collective-permute-start(bf16[512,512]{0,1:T(8,128)(2,1)} %pad_maximum_fusion.2), channel_id=1, source_target_pairs={{0,4},{4,8},{8,12},{1,5},{5,9},{9,13},{2,6},{6,10},{10,14},{3,7},{... | collective-permute-start | bytes 1572872 | tf_op jit(solution)/shard_map/ppermute | solution.py:14
  210.0 9.8 copy-start.21
  211.5 44.3 %collective-permute-start.4 = (bf16[144,2,1728]{2,0,1:T(8,128)(2,1)}, bf16[144,2,1728]{2,0,1:T(8,128)(2,1)}, u32[]{:S(2)}, u32[]{:S(2)}) collective-permute-start(bf16[144,2,1728]{2,0,1:T(8,128)(2,1)} %collective-permute-done.2), channel_id=1, source_target_pairs={{0,28},{4,0},{8,4},{12,8},{16,12},{20,16},{24,20},{28,24},{1,29},{... | collective-permute-start | bytes 2985992 | tf_op jit(solution)/shard_map/ppermute | solution.py:162
  215.3 40.5 %collective-permute-start.7 = (bf16[144,2,1728]{2,0,1:T(8,128)(2,1)}, bf16[144,2,1728]{2,0,1:T(8,128)(2,1)}, u32[]{:S(2)}, u32[]{:S(2)}) collective-permute-start(bf16[144,2,1728]{2,0,1:T(8,128)(2,1)} %collective-permute-done.5), channel_id=1, source_target_pairs={{0,4},{4,8},{8,12},{12,16},{16,20},{20,24},{24,28},{28,0},{1,5},{5... | collective-permute-start | bytes 2985992 | tf_op jit(solution)/shard_map/ppermute | solution.py:160
  222.5 128.5 %all-gather.8.cloned.1.call-start = ((), (), s32[]{:S(2)}) async-start(), calls=%async_computation.9 | async-start | bytes 4644864 | tf_op jit(solution)/shard_map/all_gather | solution.py:184
  223.2 170.4 %all-reduce.15.cloned.1.call-start = ((), (), s32[]{:S(2)}) async-start(), calls=%async_computation.10 | async-start | bytes 2359296 | tf_op jit(solution)/shard_map/psum | solution.py:182
  255.8 56.8 %collective-permute-start.6 = (bf16[144,2,1728]{2,0,1:T(8,128)(2,1)}, bf16[144,2,1728]{2,0,1:T(8,128)(2,1)}, u32[]{:S(2)}, u32[]{:S(2)}) collective-permute-start(bf16[144,2,1728]{2,0,1:T(8,128)(2,1)} %collective-permute-done.4), channel_id=1, source_target_pairs={{0,28},{4,0},{8,4},{12,8},{16,12},{20,16},{24,20},{28,24},{1,29},{... | collective-permute-start | bytes 2985992 | tf_op jit(solution)/shard_map/ppermute | solution.py:162
  255.8 62.3 %collective-permute-start.8 = (bf16[144,2,1728]{2,0,1:T(8,128)(2,1)}, bf16[144,2,1728]{2,0,1:T(8,128)(2,1)}, u32[]{:S(2)}, u32[]{:S(2)}) collective-permute-start(bf16[144,2,1728]{2,0,1:T(8,128)(2,1)} %collective-permute-done.7), channel_id=1, source_target_pairs={{0,4},{4,8},{8,12},{12,16},{16,20},{20,24},{24,28},{28,0},{1,5},{5... | collective-permute-start | bytes 2985992 | tf_op jit(solution)/shard_map/ppermute | solution.py:160
  281.7 36.4 %copy-start.7 = (bf16[512,1152]{1,0:T(8,128)(2,1)}, bf16[512,1152]{1,0:T(8,128)(2,1)S(1)}, u32[]{:S(2)}) copy-start(bf16[512,1152]{1,0:T(8,128)(2,1)S(1)} %multiply_convert_fusion.1) | copy-start | bytes 3538948
  344.2 13.8 %copy-start.76 = (f32[512]{0:T(512)S(1)}, f32[512]{0:T(512)}, u32[]{:S(2)}) copy-start(f32[512]{0:T(512)} %copy-done.75) | copy-start | bytes 6148
  344.2 13.8 %copy-start.78 = (f32[512]{0:T(512)S(1)}, f32[512]{0:T(512)}, u32[]{:S(2)}) copy-start(f32[512]{0:T(512)} %copy-done.77) | copy-start | bytes 6148
  357.3 161.9 %all-gather.10.cloned.1.call-start = ((), (), s32[]{:S(2)}) async-start(), calls=%async_computation.11 | async-start | bytes 9289728 | tf_op jit(solution)/shard_map/all_gather | solution.py:203
  357.9 208.5 %all-reduce.17.cloned.1.call-start = ((), (), s32[]{:S(2)}) async-start(), calls=%async_computation.12 | async-start | bytes 2359296 | tf_op jit(solution)/shard_map/psum | solution.py:206
  530.6 110.3 %all-reduce.19.cloned.1.call-start = ((), (), s32[]{:S(2)}) async-start(), calls=%async_computation.20 | async-start | bytes 3407872 | tf_op jit(solution)/shard_map/psum | solution.py:267
  579.9 15.5 %collective-permute-start.9 = (bf16[512,512]{0,1:T(8,128)(2,1)S(1)}, bf16[512,512]{0,1:T(8,128)(2,1)S(1)}, u32[]{:S(2)}, u32[]{:S(2)}) collective-permute-start(bf16[512,512]{0,1:T(8,128)(2,1)S(1)} %fusion.66), channel_id=1, source_target_pairs={{4,0},{8,4},{12,8},{5,1},{9,5},{13,9},{6,2},{10,6},{14,10},{7,3},{... | collective-permute-start | bytes 1572872 | tf_op jit(solution)/shard_map/ppermute | solution.py:14
  596.4 135.9 %reduce-scatter.26.cloned.1.call-start = ((), (), s32[]{:S(2)}) async-start(), calls=%async_computation.18 | async-start | bytes 4644864
  608.7 214.7 %reduce-scatter.28.cloned.1.call-start = ((), (), s32[]{:S(2)}) async-start(), calls=%async_computation.19 | async-start | bytes 4644864
  615.3 299.1 %reduce-scatter.20.cloned.1.call-start = ((), (), s32[]{:S(2)}) async-start(), calls=%async_computation.15 | async-start | bytes 4644864 | tf_op jit(solution)/shard_map/reduce_scatter | solution.py:215
  622.9 357.5 %reduce-scatter.24.cloned.1.call-start = ((), (), s32[]{:S(2)}) async-start(), calls=%async_computation.17 | async-start | bytes 73728
  631.6 11.1 copy-start.83
  631.6 12.2 %copy-start.9 = (f32[512,512]{0,1:T(8,128)S(1)}, f32[512,512]{0,1:T(8,128)}, u32[]{:S(2)}) copy-start(f32[512,512]{0,1:T(8,128)} %copy-done.8) | copy-start | bytes 3145732
  631.6 12.2 %copy-start.46 = (f32[512]{0:T(512)S(1)}, f32[512]{0:T(512)}, u32[]{:S(2)}) copy-start(f32[512]{0:T(512)} %copy-done.45) | copy-start | bytes 6148
  631.6 12.2 %copy-start.70 = (f32[1,256]{1,0:T(1,128)S(1)}, f32[1,256]{1,0:T(1,128)}, u32[]{:S(2)}) copy-start(f32[1,256]{1,0:T(1,128)} %copy-done.69) | copy-start | bytes 3076
  633.1 11.7 copy-start.59
  650.1 392.4 %reduce-scatter.22.cloned.1.call-start = ((), (), s32[]{:S(2)}) async-start(), calls=%async_computation.16 | async-start | bytes 331776
  651.1 458.6 %reduce-scatter.16.cloned.1.call-start = ((), (), s32[]{:S(2)}) async-start(), calls=%async_computation.13 | async-start | bytes 1327104 | tf_op jit(solution)/shard_map/reduce_scatter | solution.py:282
  652.3 524.3 %reduce-scatter.18.cloned.1.call-start = ((), (), s32[]{:S(2)}) async-start(), calls=%async_computation.14 | async-start | bytes 1327104 | tf_op jit(solution)/shard_map/reduce_scatter | solution.py:300
  827.0 89.5 %copy-start.57 = (f32[512]{0:T(512)S(1)}, f32[512]{0:T(512)}, u32[]{:S(2)}) copy-start(f32[512]{0:T(512)} %copy-done.56) | copy-start | bytes 6148
  827.0 90.1 %copy-start.5 = (f32[512,1152]{1,0:T(8,128)S(1)}, f32[512,1152]{1,0:T(8,128)}, u32[]{:S(2)}) copy-start(f32[512,1152]{1,0:T(8,128)} %copy-done.4) | copy-start | bytes 7077892
  (62 other events, 192.1 us)
Sparse Core Ops, SparseCore 0:
  14.9 58.7 all-gather.5
  222.6 54.1 all-reduce.12
  278.8 72.0 all-gather.7
  357.4 36.1 all-reduce.14
  396.2 122.9 all-gather.9
  530.7 35.6 all-reduce.16
  596.5 44.2 all-reduce.18
  644.4 87.8 reduce-scatter.25
  735.9 87.5 reduce-scatter.27
  826.9 87.4 reduce-scatter.19
  918.4 62.0 reduce-scatter.23
  984.2 58.2 reduce-scatter.21
  1045.8 63.8 reduce-scatter.15
  1112.9 63.6 reduce-scatter.17
